TPU v7x, 32 devices: a whole 2x2x4 slice. The times are simulated.
32 devices in a mesh: dp: 8 (over z, y), head: 4 (over x, core).
Axes of the slice: x: 2, y: 2, z: 4, core: 2. Of those that a mesh axis runs over, the one named last changes fastest.
Arguments:
- hidden: bfloat16 [1792, 16384], P('dp', 'head'), may hold values from -6 to 6
- norm_gain: float32 [16384], replicated, may hold values from 0.25 to 1.75
- query_weight: bfloat16 [16384, 2048], P('dp', 'head'), may hold values from -0.046875 to 0.046875
- kv_weight: bfloat16 [16384, 512], P(None, 'head'), may hold values from -0.046875 to 0.046875
- lengths: int32 [8, 2], replicated, may hold values from 28 to 112
- route_plan: int32 [8, 3], replicated, may hold values from 0 to 1
Outputs:
- attended: bfloat16 [1792, 2048], P('dp', 'head')
- fluctuation: float32 [2048], P('head')
- gram_matrix: float32 [8192, 8192], P('head', 'dp')
All inputs are finite; a program needn't handle non-finite values.
Results may differ from a plain program's by a relative error of at most 0.0085.
Values may be sent and summed in bfloat16 or wider, within the bound.
No kernel may reach another device: no remote copies, remote signals or barrier semaphores. Data moves between devices by JAX's collectives and lax.ppermute only.
A program may use at most 128 MiB of HBM per device.

v0:
```python
import jax
import jax.numpy as jnp
from jax import lax
from jax.sharding import PartitionSpec as P


GW = 8192

rope_theta = 500000.0
norm_eps = 1e-05


def take(array, index, axis=0):
    return lax.dynamic_index_in_dim(array, index, axis, keepdims=False)


def partner_2(value, axis, stride):
    mask = 2**stride
    pairs = [(source, source ^ mask) for source in range(lax.axis_size(axis))]
    return lax.ppermute(value, axis, pairs)


def send(value, target):
    dp_count = lax.axis_size("dp")
    head_count = lax.axis_size("head")
    pairs = []
    for d in range(dp_count):
        for h in range(head_count):
            to = target(d, h)
            if to is not None:
                pairs.append((d * head_count + h, to[0] * head_count + to[1]))
    return lax.ppermute(value, ("dp", "head"), pairs)


def add_up(value, axis):
    stride = 0
    while 2**stride < lax.axis_size(axis):
        value = value + partner_2(value, axis, stride)
        stride += 1
    return value


def rotate(values_in, cosines, sines):
    middle = values_in.shape[-1] // 2
    front_half = values_in[..., :middle]
    back_half = values_in[..., middle:]
    return jnp.concatenate(
        [front_half * cosines - back_half * sines, back_half * cosines + front_half * sines],
        axis=-1,
    )


def tie(value, after):
    return lax.optimization_barrier((value, after))[0]


def scale_by(values, factor, gain):
    return (values.astype(jnp.float32) * factor[:, None] * gain[None, :]).astype(jnp.bfloat16)


def norm_factor(local, width, seq_lengths, length_max):
    mean = add_up(local, "head") / width
    positions = jnp.arange(length_max, dtype=jnp.int32)
    usable = (positions[None, :] < seq_lengths[:, None]).reshape(mean.shape)
    return jnp.where(usable, lax.rsqrt(mean + norm_eps), 0.0)


def attend(query, keys, values, seq_lengths, length_max):
    slot_count = seq_lengths.shape[0]
    row_count, query_width = query.shape
    head_dim = keys.shape[1]
    heads_here = query_width // head_dim
    positions = jnp.arange(length_max, dtype=jnp.int32)
    usable = positions[None, :] < seq_lengths[:, None]
    middle = head_dim // 2
    frequency = rope_theta ** (-(2.0 * jnp.arange(middle, dtype=jnp.float32) / head_dim))
    angles = jnp.tile(positions.astype(jnp.float32), slot_count)[:, None] * frequency[None, :]
    cosines = jnp.cos(angles)
    sines = jnp.sin(angles)
    rotated_query = rotate(
        query.reshape(row_count, heads_here, head_dim), cosines[:, None, :], sines[:, None, :]
    ).astype(jnp.bfloat16)
    rotated_keys = rotate(keys.astype(jnp.float32), cosines, sines).astype(jnp.bfloat16)
    query_blocks = rotated_query.reshape(slot_count, length_max, heads_here, head_dim)
    key_blocks = rotated_keys.reshape(slot_count, length_max, head_dim)
    value_blocks = values.reshape(slot_count, length_max, head_dim)
    scores = jnp.einsum(
        "slqh,smh->sqlm", query_blocks, key_blocks, preferred_element_type=jnp.float32
    ) * head_dim ** (-0.5)
    allowed = (positions[None, :, None] >= positions[None, None, :]) & usable[:, None, :]
    exponent = jnp.where(allowed[:, None], jnp.exp(scores), 0.0)
    attn_probs = (exponent / jnp.sum(exponent, axis=-1, keepdims=True)).astype(jnp.bfloat16)
    mixed_out = jnp.einsum(
        "sqlm,smh->slqh", attn_probs, value_blocks, preferred_element_type=jnp.float32
    )
    return jnp.where(
        usable.reshape(row_count)[:, None], mixed_out.reshape(row_count, query_width), 0.0
    ).astype(jnp.bfloat16)


def trade(sequences, route_plan):
    group_index = lax.axis_index("dp")
    for round_bit in range(route_plan.shape[1]):
        leaving_here = take(route_plan[:, round_bit], group_index)
        arrived = partner_2(take(sequences, leaving_here), "dp", round_bit)
        sequences = lax.dynamic_update_index_in_dim(sequences, arrived, leaving_here, 0)
    return sequences


def keys_values(own_part):
    other_part = partner_2(own_part, "head", 0)
    leading = lax.axis_index("head") % 2 == 0
    keys = jnp.where(leading, own_part, other_part)
    values = jnp.where(leading, other_part, own_part)
    return keys, values


def project_any(hidden, norm_gain, query_weight, kv_weight, factor):
    whole = lax.all_gather(hidden, "head", axis=1, tiled=True)
    normed = scale_by(whole, factor, norm_gain)
    query = jnp.dot(
        normed,
        lax.all_gather(query_weight, "dp", axis=0, tiled=True),
        preferred_element_type=jnp.float32,
    )
    own_part = jnp.dot(normed, kv_weight, preferred_element_type=jnp.float32).astype(jnp.bfloat16)
    keys, values = keys_values(own_part)
    return query, keys, values, normed


def gram_any(normed, counted):
    head_count = lax.axis_size("head")
    columns = lax.all_to_all(normed[:, :GW], "dp", split_axis=1, concat_axis=0, tiled=True)
    span = GW // head_count
    own_rows = lax.dynamic_slice_in_dim(normed, lax.axis_index("head") * span, span, 1)
    rows = lax.all_gather(own_rows, "dp", axis=0, tiled=True)
    return (
        lax.dot_general(
            rows, columns, (((0,), (0,)), ((), ())), preferred_element_type=jnp.float32
        )
        / counted
    )


def flip_x(value):
    return send(value, lambda d, h: (d, h ^ 2))


def flip_core(value):
    return send(value, lambda d, h: (d, h ^ 1))


def flip_y(value):
    return send(value, lambda d, h: (d ^ 1, h))


def project_planes(keep, came, query_weight, other_rows, kv_weight):
    d, h = lax.axis_index("dp"), lax.axis_index("head")
    z, y, x, c = d // 2, d % 2, h // 2, h % 2
    w, p = z // 2, z % 2
    cols = keep.shape[1]
    weight = jnp.where(
        y == 0,
        jnp.concatenate([query_weight, other_rows]),
        jnp.concatenate([other_rows, query_weight]),
    )
    kv_rows = lax.dynamic_slice_in_dim(kv_weight, z * cols, cols, 0)
    matrix = jnp.concatenate([weight, kv_rows, flip_core(weight), flip_core(kv_rows)], axis=1)
    matrix = lax.optimization_barrier(matrix)
    half = matrix.shape[1] // 2
    total = None
    for e in range(2):

        def to_plane(d, h, e=e):
            z, y, x, c = d // 2, d % 2, h // 2, h % 2
            return 2 * (2 * ((z // 2) ^ e) + c) + y, 2 * x + z % 2

        def kept(d, h, e=e, to_plane=to_plane):
            return to_plane(d, h) if ((d // 4) ^ e) == h // 2 else None

        def passed(d, h, e=e, to_plane=to_plane):
            return to_plane(d, h) if ((d // 4) ^ e) != h // 2 else None

        mine = jnp.where(w == x, send(keep, kept), send(came, passed))
        tokens = jnp.concatenate([mine, flip_x(mine)])
        product = jnp.dot(tokens, matrix, preferred_element_type=jnp.float32)
        product = product.astype(jnp.bfloat16)
        for f in range(2):
            chunk = jnp.where((p ^ f) == c, product[:, :half], product[:, half:])

            def to_group(d, h, e=e, f=f):
                z, y, x, c = d // 2, d % 2, h // 2, h % 2
                return 2 * (2 * ((z // 2) ^ e) + c) + y, 2 * x + ((z % 2) ^ f)

            part = send(chunk, to_group).astype(jnp.float32)
            total = part if total is None else total + part
    return total


def arrival(up, down, z, step):
    last = len(up) - 1
    block = None
    for plane in range(last + 1):
        order = []
        for k in range(1, last + 1):
            if k <= plane:
                order.append(up[k])
            if k <= last - plane:
                order.append(down[k])
        mine = order[step - 1]
        block = mine if block is None else jnp.where(z == plane, mine, block)
    return block


def gram_planes(block, counted):
    dp_count = lax.axis_size("dp")
    last = dp_count // 2 - 1
    d, h = lax.axis_index("dp"), lax.axis_index("head")
    z, y = d // 2, d % 2
    col_span = GW // dp_count
    up, down = [block], [block]
    for step in range(1, last + 1):

        def rise(d, h, step=step):
            return (d + 2, h) if step - 1 <= d // 2 < last else None

        def sink(d, h, step=step):
            return (d - 2, h) if 0 < d // 2 <= last + 1 - step else None

        up.append(send(up[-1], rise))
        down.append(send(down[-1], sink))

    def dot(parts_a, parts_b):
        return lax.dot_general(
            jnp.concatenate(parts_a),
            jnp.concatenate(parts_b),
            (((0,), (0,)), ((), ())),
            preferred_element_type=jnp.float32,
        )

    row_parts, col_parts = [], []
    for step in range(last + 1):
        if step:
            block = arrival(up, down, tie(z, block), step)
        pair = jnp.concatenate([block, flip_y(block)])
        cut = lax.dynamic_slice_in_dim(pair, y * col_span, col_span, 1)
        if step == last:
            early = dot(row_parts, col_parts)
            early = lax.optimization_barrier(early)
        across = send(cut, lambda d, h: (d, h ^ 2) if h == d // 2 else None)
        have = jnp.where(h == z, cut, across)
        twin = send(have, lambda d, h: (d, h ^ 1) if h in (d // 2, (d // 2) ^ 2) else None)
        row_parts.append(pair)
        col_parts.append(jnp.where((h == z) | (h == (z ^ 2)), have, twin))
    return (dot(row_parts[-1:], col_parts[-1:]) + early) / counted


def planes(hidden, norm_gain, query_weight, kv_weight, own_lengths, length_max, counted):
    h = lax.axis_index("head")
    x = h // 2
    rows, cols = hidden.shape
    slot_count = rows // length_max
    span = cols // 2
    sequences = hidden.reshape(slot_count, length_max, cols)
    raw = flip_x(take(sequences, 1 - x))
    other_rows = flip_y(query_weight)
    widened = hidden.astype(jnp.float32)
    local = jnp.sum(widened * widened, axis=1)
    factor = norm_factor(local, cols * lax.axis_size("head"), own_lengths, length_max)
    slot_factor = take(factor.reshape(slot_count, length_max), x)
    keep = scale_by(
        take(sequences, x), slot_factor, lax.dynamic_slice_in_dim(norm_gain, h * cols, cols)
    )
    came = scale_by(
        raw, tie(slot_factor, keep), lax.dynamic_slice_in_dim(norm_gain, (h ^ 2) * cols, cols)
    )
    first, second = hidden[:, :span], hidden[:, span:]
    late = tie(h, raw)
    near = send(jnp.where(late == 0, second, first), lambda d, h: (d, h + 1) if h < 2 else None)
    far = send(jnp.where(late == 1, second, first), lambda d, h: (d, 3) if h == 1 else None)
    total = project_planes(keep, came, query_weight, other_rows, kv_weight)
    block = scale_by(
        jnp.where(h == 0, first, jnp.where(h == 3, far, near)),
        factor,
        lax.dynamic_slice_in_dim(norm_gain, h * span, span),
    )
    return total, gram_planes(block, counted)


def whole_step(hidden, norm_gain, query_weight, kv_weight, lengths, route_plan):
    dp_count = lax.axis_size("dp")
    head_count = lax.axis_size("head")
    group_index = lax.axis_index("dp")
    head_index = lax.axis_index("head")
    slot_count = lengths.shape[1]
    rows, cols = hidden.shape
    length_max = rows // slot_count
    query_width = query_weight.shape[1]
    counted = jnp.sum(lengths).astype(jnp.float32)
    own_lengths = take(lengths, group_index)
    by_planes = (
        plane_mesh(dp_count, head_count)
        and slot_count == 2
        and GW == 2 * cols
        and cols == 2 * query_weight.shape[0]
    )
    if by_planes:
        swapped = head_index // 2 == 1
        total, gram_matrix = planes(
            hidden, norm_gain, query_weight, kv_weight, own_lengths, length_max, counted
        )
        seq_lengths = jnp.where(swapped, own_lengths[::-1], own_lengths)
        query = total[:, :query_width]
        own_part = total[:, query_width:].astype(jnp.bfloat16)
        keys, values = keys_values(own_part)
    else:
        widened = hidden.astype(jnp.float32)
        factor = norm_factor(
            jnp.sum(widened * widened, axis=1), cols * head_count, own_lengths, length_max
        )
        query, keys, values, normed = project_any(
            hidden, norm_gain, query_weight, kv_weight, factor
        )
        seq_lengths = own_lengths
        gram_matrix = gram_any(normed, counted)
    attended = attend(query, keys, values, seq_lengths, length_max)
    spread_in = attended.astype(jnp.float32)
    summed, squared = add_up(
        jnp.stack([jnp.sum(spread_in, axis=0), jnp.sum(spread_in * spread_in, axis=0)]), "dp"
    )
    fluctuation = (squared - summed * summed / counted) / (counted - 1.0)
    slots = attended.reshape(slot_count, length_max, query_width)
    if by_planes:
        slots = jnp.where(swapped, slots[::-1], slots)
    attended = trade(slots, route_plan).reshape(rows, query_width)
    return (attended, fluctuation, gram_matrix)


def plane_mesh(dp_count, head_count):
    return head_count == 4 and dp_count == 2 * head_count


def solution(mesh):
    return jax.shard_map(
        whole_step,
        mesh=mesh,
        in_specs=(P("dp", "head"), P(), P("dp", "head"), P(None, "head"), P(), P()),
        out_specs=(P("dp", "head"), P("head"), P("head", "dp")),
        check_vma=False,
    )
```

profile of v0, /device:TPU:0, one launch (start us, length us, event | category | flops | bytes accessed | tf_op | source)
XLA Modules:
  0.0 283.5 jit_solution(10779470613776545692)
XLA Ops:
  0.7 3.1 %collective-permute-start.6 = (bf16[2048,512]{1,0:T(8,128)(2,1)}, bf16[2048,512]{1,0:T(8,128)(2,1)}, u32[]{:S(2)}, u32[]{:S(2)}) collective-permute-start(bf16[2048,512]{1,0:T(8,128)(2,1)} %param.8), channel_id=1, source_target_pairs={{0,4},{1,5},{2,6},{3,7},{4,0},{5,1},{6,2},{7,3},{8,12},{9,13},{10,... | collective-permute-start | bytes 6291464 | tf_op jit(solution)/shard_map/ppermute | solution.py:32
  5.8 2.2 dynamic-slice_bitcast_fusion
  19.2 11.7 %collective-permute-done.1 = f32[224]{0:T(256)S(1)} collective-permute-done((f32[224]{0:T(256)S(1)}, f32[224]{0:T(256)S(1)}, u32[]{:S(2)}, u32[]{:S(2)}) %collective-permute-start.1) | collective-permute-done | bytes 928 | tf_op jit(solution)/shard_map/ppermute | solution.py:20
  34.5 9.6 %collective-permute-start.24 = (bf16[224,2048]{1,0:T(8,128)(2,1)S(1)}, bf16[224,2048]{1,0:T(8,128)(2,1)S(1)}, u32[]{:S(2)}, u32[]{:S(2)}) collective-permute-start(bf16[224,2048]{1,0:T(8,128)(2,1)S(1)} %get-tuple-element.21), channel_id=1, source_target_pairs={{0,1},{1,2},{4,5},{5,6},{8,9},{9,10},{12,13},{13,14},{16,17},{17,1... | collective-permute-start | bytes 2752520 | tf_op jit(solution)/shard_map/ppermute | solution.py:32
  47.1 8.3 %collective-permute-start.2 = (bf16[112,4096]{1,0:T(8,128)(2,1)}, bf16[112,4096]{1,0:T(8,128)(2,1)}, u32[]{:S(2)}, u32[]{:S(2)}) collective-permute-start(bf16[112,4096]{1,0:T(8,128)(2,1)} %fusion.13), channel_id=1, source_target_pairs={{0,0},{1,8},{4,4},{5,12},{8,1},{9,9},{12,5},{13,13},{18,18},{19,26... | collective-permute-start | bytes 2752520 | tf_op jit(solution)/shard_map/ppermute | solution.py:32
  57.7 20.1 %collective-permute-done.11 = bf16[112,4096]{1,0:T(8,128)(2,1)} collective-permute-done((bf16[112,4096]{1,0:T(8,128)(2,1)}, bf16[112,4096]{1,0:T(8,128)(2,1)}, u32[]{:S(2)}, u32[]{:S(2)}) %collective-permute-start.11) | collective-permute-done | bytes 917536 | tf_op jit(solution)/shard_map/ppermute | solution.py:32
  77.8 3.1 %collective-permute-start.25 = (bf16[224,2048]{1,0:T(8,128)(2,1)}, bf16[224,2048]{1,0:T(8,128)(2,1)}, u32[]{:S(2)}, u32[]{:S(2)}) collective-permute-start(bf16[224,2048]{1,0:T(8,128)(2,1)} %get-tuple-element.20), channel_id=1, source_target_pairs={{0,8},{1,9},{2,10},{3,11},{4,12},{5,13},{6,14},{7,15},{8,16},{9,17... | collective-permute-start | bytes 2752520 | tf_op jit(solution)/shard_map/ppermute | solution.py:32
  82.2 2.2 broadcast_select_fusion.9
  85.2 5.6 %maximum_select_fusion = bf16[4096,512]{1,0:T(8,128)(2,1)} fusion(bf16[2048,512]{1,0:T(8,128)(2,1)} %collective-permute-done.6, bf16[2048,512]{1,0:T(8,128)(2,1)} %param.8, pred[]{:T(512)S(6)} %eq.86), kind=kLoop, calls=%fused_computation.2 | loop fusion | flops 18874368 | bytes 8388609 | tf_op jit(solution)/shard_map/jit(_where)/select_n | solution.py:162
  91.9 3.5 %collective-permute-done.25 = bf16[224,2048]{1,0:T(8,128)(2,1)} collective-permute-done((bf16[224,2048]{1,0:T(8,128)(2,1)}, bf16[224,2048]{1,0:T(8,128)(2,1)}, u32[]{:S(2)}, u32[]{:S(2)}) %collective-permute-start.25) | collective-permute-done | bytes 917536 | tf_op jit(solution)/shard_map/ppermute | solution.py:32
  95.4 11.9 %collective-permute-done.26 = bf16[224,2048]{1,0:T(8,128)(2,1)S(1)} collective-permute-done((bf16[224,2048]{1,0:T(8,128)(2,1)}, bf16[224,2048]{1,0:T(8,128)(2,1)S(1)}, u32[]{:S(2)}, u32[]{:S(2)}) %collective-permute-start.26) | collective-permute-done | bytes 917536 | tf_op jit(solution)/shard_map/ppermute | solution.py:32
  107.2 3.2 %constant_dynamic-update-slice_fusion.3 = (bf16[1344,2048]{1,0:T(8,128)(2,1)}, bf16[224,2048]{1,0:T(8,128)(2,1)}) fusion(bf16[1344,2048]{1,0:T(8,128)(2,1)} %constant_dynamic-update-slice_fusion.4, bf16[224,2048]{1,0:T(8,128)(2,1)} %collective-permute-done.25, bf16[224,2048]{1,0:T(8,128)(2,1)S(1)} %collective-permute-done.26, pred[]{:T(512)S(6)} %eq.94, ...), kind=kLoop, calls=%fused_computation.100 | loop fusion | flops 1376256 | bytes 3670019
  113.8 2.2 broadcast_select_fusion.10
  116.0 2.1 fusion.20
  118.1 2.2 collective-permute-start.37
  122.0 18.1 %collective-permute-done.28 = bf16[224,2048]{1,0:T(8,128)(2,1)} collective-permute-done((bf16[224,2048]{1,0:T(8,128)(2,1)}, bf16[224,2048]{1,0:T(8,128)(2,1)}, u32[]{:S(2)}, u32[]{:S(2)}) %collective-permute-start.28) | collective-permute-done | bytes 917536 | tf_op jit(solution)/shard_map/ppermute | solution.py:32
  142.4 3.0 %constant_dynamic-update-slice_fusion.1 = (bf16[1344,2048]{1,0:T(8,128)(2,1)}, bf16[224,2048]{1,0:T(8,128)(2,1)}) fusion(bf16[1344,2048]{1,0:T(8,128)(2,1)} %constant_dynamic-update-slice_fusion.2, bf16[224,2048]{1,0:T(8,128)(2,1)} %collective-permute-done.27, bf16[224,2048]{1,0:T(8,128)(2,1)S(1)} %copy-done.5, ...), kind=kLoop, calls=%fused_computation.98 | loop fusion | flops 1376256 | bytes 4587523
  151.7 13.3 %collective-permute-done.30 = bf16[224,2048]{1,0:T(8,128)(2,1)} collective-permute-done((bf16[224,2048]{1,0:T(8,128)(2,1)}, bf16[224,2048]{1,0:T(8,128)(2,1)}, u32[]{:S(2)}, u32[]{:S(2)}) %collective-permute-start.30) | collective-permute-done | bytes 917536 | tf_op jit(solution)/shard_map/ppermute | solution.py:32
  176.0 14.2 %collective-permute-done.31 = bf16[224,2048]{1,0:T(8,128)(2,1)S(1)} collective-permute-done((bf16[224,2048]{1,0:T(8,128)(2,1)S(1)}, bf16[224,2048]{1,0:T(8,128)(2,1)S(1)}, u32[]{:S(2)}, u32[]{:S(2)}) %collective-permute-start.31) | collective-permute-done | bytes 917536 | tf_op jit(solution)/shard_map/ppermute | solution.py:32
  190.4 2.1 collective-permute-start.5
  197.0 5.0 %pad_maximum_fusion = bf16[4096,1280]{1,0:T(8,128)(2,1)S(1)} fusion(bf16[4096,128]{1,0:T(8,128)(2,1)S(1)} %collective-permute-done.8, bf16[4096,512]{1,0:T(8,128)(2,1)} %collective-permute-done.7, bf16[4096,128]{1,0:T(8,128)(2,1)S(1)} %constant_dynamic-slice_fusion.3, bf16[4096,512]{1,0:T(8,128)(2,1)} %maximum_select_fusion), kind=kLoop, calls=%fused_computation | loop fusion | flops 41943040 | bytes 20971520 | tf_op jit(solution)/shard_map/concatenate | solution.py:168
  202.0 11.4 %collective-permute-done.13 = bf16[112,4096]{1,0:T(8,128)(2,1)S(1)} collective-permute-done((bf16[112,4096]{1,0:T(8,128)(2,1)S(1)}, bf16[112,4096]{1,0:T(8,128)(2,1)S(1)}, u32[]{:S(2)}, u32[]{:S(2)}) %collective-permute-start.13) | collective-permute-done | bytes 917536 | tf_op jit(solution)/shard_map/ppermute | solution.py:32
  213.5 2.6 convolution_convert_fusion
  218.0 12.9 %collective-permute-done.5 = bf16[112,4096]{1,0:T(8,128)(2,1)S(1)} collective-permute-done((bf16[112,4096]{1,0:T(8,128)(2,1)S(1)}, bf16[112,4096]{1,0:T(8,128)(2,1)S(1)}, u32[]{:S(2)}, u32[]{:S(2)}) %collective-permute-start.5) | collective-permute-done | bytes 917536 | tf_op jit(solution)/shard_map/ppermute | solution.py:32
  230.9 2.6 convolution_convert_fusion.1
  233.6 4.9 %collective-permute-done.32 = bf16[448,1024]{1,0:T(8,128)(2,1)S(1)} collective-permute-done((bf16[448,1024]{1,0:T(8,128)(2,1)S(1)}, bf16[448,1024]{1,0:T(8,128)(2,1)S(1)}, u32[]{:S(2)}, u32[]{:S(2)}) %collective-permute-start.32) | collective-permute-done | bytes 917536 | tf_op jit(solution)/shard_map/ppermute | solution.py:32
  240.3 2.2 collective-permute-start.33
  243.1 3.0 %collective-permute-start.16 = (bf16[224,128]{1,0:T(8,128)(2,1)S(1)}, bf16[224,128]{1,0:T(8,128)(2,1)S(1)}, u32[]{:S(2)}, u32[]{:S(2)}) collective-permute-start(bf16[224,128]{1,0:T(8,128)(2,1)S(1)} %slice.97), channel_id=1, source_target_pairs={{0,1},{1,0},{2,3},{3,2},{4,5},{5,4},{6,7},{7,6},{8,9},{9,8},{10,11... | collective-permute-start | bytes 172040 | tf_op jit(solution)/shard_map/ppermute | solution.py:20
  258.4 2.1 collective-permute-start.18
  260.4 9.1 %fusion = f32[2048,1024]{1,0:T(8,128)S(1)} fusion(bf16[1344,2048]{1,0:T(8,128)(2,1)} %constant_dynamic-update-slice_fusion, bf16[448,1024]{1,0:T(8,128)(2,1)} %broadcast_select_fusion.4, bf16[448,1024]{1,0:T(8,128)(2,1)S(1)} %copy-done.11, bf16[448,1024]{1,0:T(8,128)(2,1)S(1)} %copy-done.9), kind=kOutput, calls=%fused_computation.4 | convolution fusion | flops 5645402112 | bytes 16646144 | tf_op jit(solution)/shard_map/dot_general | solution.py:234
  270.8 5.4 %collective-permute-done.19 = bf16[112,512]{1,0:T(8,128)(2,1)S(1)} collective-permute-done((bf16[112,512]{1,0:T(8,128)(2,1)S(1)}, bf16[112,512]{1,0:T(8,128)(2,1)S(1)}, u32[]{:S(2)}, u32[]{:S(2)}) %collective-permute-start.19) | collective-permute-done | bytes 114720 | tf_op jit(solution)/shard_map/ppermute | solution.py:20
  276.3 7.2 %add_divide_fusion = f32[2048,1024]{1,0:T(8,128)} fusion(f32[2048,1024]{1,0:T(8,128)S(1)} %fusion, f32[]{:T(128)S(6)} %convert_element_type.108, bf16[224,2048]{1,0:T(8,128)(2,1)S(1)} %copy-done.8, bf16[224,2048]{1,0:T(8,128)(2,1)S(1)} %copy-done.3, bf16[448,1024]{1,0:T(8,128)(2,1)} %broadcast_select_fusion.3, ...), kind=kOutput, calls=%fused_computation.1 | convolution fusion | flops 1887371264 | bytes 20447236 | tf_op jit(solution)/shard_map/dot_general | solution.py:234
  (173 shorter events, 65.4 us)
Async XLA Ops:
  0.7 83.8 %collective-permute-start.6 = (bf16[2048,512]{1,0:T(8,128)(2,1)}, bf16[2048,512]{1,0:T(8,128)(2,1)}, u32[]{:S(2)}, u32[]{:S(2)}) collective-permute-start(bf16[2048,512]{1,0:T(8,128)(2,1)} %param.8), channel_id=1, source_target_pairs={{0,4},{1,5},{2,6},{3,7},{4,0},{5,1},{6,2},{7,3},{8,12},{9,13},{10,... | collective-permute-start | bytes 6291464 | tf_op jit(solution)/shard_map/ppermute | solution.py:32
  7.9 25.6 %collective-permute-start.3 = (bf16[112,4096]{1,0:T(8,128)(2,1)}, bf16[112,4096]{1,0:T(8,128)(2,1)S(1)}, u32[]{:S(2)}, u32[]{:S(2)}) collective-permute-start(bf16[112,4096]{1,0:T(8,128)(2,1)} %dynamic-slice_bitcast_fusion), channel_id=1, source_target_pairs={{0,2},{1,3},{2,0},{3,1},{4,6},{5,7},{6,4},{7,5},{8,10},{9,11},{10,... | collective-permute-start | bytes 2752520 | tf_op jit(solution)/shard_map/ppermute | solution.py:32
  15.9 15.0 %collective-permute-start.1 = (f32[224]{0:T(256)S(1)}, f32[224]{0:T(256)S(1)}, u32[]{:S(2)}, u32[]{:S(2)}) collective-permute-start(f32[224]{0:T(256)S(1)} %add.109), channel_id=1, source_target_pairs={{0,2},{1,3},{2,0},{3,1},{4,6},{5,7},{6,4},{7,5},{8,10},{9,11},{10,... | collective-permute-start | bytes 2696 | tf_op jit(solution)/shard_map/ppermute | solution.py:20
  32.3 45.5 %collective-permute-start.11 = (bf16[112,4096]{1,0:T(8,128)(2,1)}, bf16[112,4096]{1,0:T(8,128)(2,1)}, u32[]{:S(2)}, u32[]{:S(2)}) collective-permute-start(bf16[112,4096]{1,0:T(8,128)(2,1)} %fusion.13), channel_id=1, source_target_pairs={{2,18},{3,26},{6,22},{7,30},{10,19},{11,27},{14,23},{15,31},{16,0}... | collective-permute-start | bytes 2752520 | tf_op jit(solution)/shard_map/ppermute | solution.py:32
  33.7 13.3 %collective-permute-start.23 = (bf16[224,2048]{1,0:T(8,128)(2,1)S(1)}, bf16[224,2048]{1,0:T(8,128)(2,1)S(1)}, u32[]{:S(2)}, u32[]{:S(2)}) collective-permute-start(bf16[224,2048]{1,0:T(8,128)(2,1)S(1)} %get-tuple-element.22), channel_id=1, source_target_pairs={{1,3},{5,7},{9,11},{13,15},{17,19},{21,23},{25,27},{29,31}} | collective-permute-start | bytes 2752520 | tf_op jit(solution)/shard_map/ppermute | solution.py:32
  34.5 20.9 %collective-permute-start.24 = (bf16[224,2048]{1,0:T(8,128)(2,1)S(1)}, bf16[224,2048]{1,0:T(8,128)(2,1)S(1)}, u32[]{:S(2)}, u32[]{:S(2)}) collective-permute-start(bf16[224,2048]{1,0:T(8,128)(2,1)S(1)} %get-tuple-element.21), channel_id=1, source_target_pairs={{0,1},{1,2},{4,5},{5,6},{8,9},{9,10},{12,13},{13,14},{16,17},{17,1... | collective-permute-start | bytes 2752520 | tf_op jit(solution)/shard_map/ppermute | solution.py:32
  44.4 36.5 %collective-permute-start.12 = (bf16[112,4096]{1,0:T(8,128)(2,1)S(1)}, bf16[112,4096]{1,0:T(8,128)(2,1)S(1)}, u32[]{:S(2)}, u32[]{:S(2)}) collective-permute-start(bf16[112,4096]{1,0:T(8,128)(2,1)S(1)} %multiply_convert_fusion.1), channel_id=1, source_target_pairs={{0,16},{1,24},{4,20},{5,28},{8,17},{9,25},{12,21},{13,29},{18,2},{... | collective-permute-start | bytes 2752520 | tf_op jit(solution)/shard_map/ppermute | solution.py:32
  47.1 65.4 %collective-permute-start.2 = (bf16[112,4096]{1,0:T(8,128)(2,1)}, bf16[112,4096]{1,0:T(8,128)(2,1)}, u32[]{:S(2)}, u32[]{:S(2)}) collective-permute-start(bf16[112,4096]{1,0:T(8,128)(2,1)} %fusion.13), channel_id=1, source_target_pairs={{0,0},{1,8},{4,4},{5,12},{8,1},{9,9},{12,5},{13,13},{18,18},{19,26... | collective-permute-start | bytes 2752520 | tf_op jit(solution)/shard_map/ppermute | solution.py:32
  57.2 33.6 %collective-permute-start.34 = (bf16[224,2048]{1,0:T(8,128)(2,1)}, bf16[224,2048]{1,0:T(8,128)(2,1)S(1)}, u32[]{:S(2)}, u32[]{:S(2)}) collective-permute-start(bf16[224,2048]{1,0:T(8,128)(2,1)} %get-tuple-element.20), channel_id=1, source_target_pairs={{0,4},{1,5},{2,6},{3,7},{4,0},{5,1},{6,2},{7,3},{8,12},{9,13},{10,... | collective-permute-start | bytes 2752520 | tf_op jit(solution)/shard_map/ppermute | solution.py:32
  77.8 17.5 %collective-permute-start.25 = (bf16[224,2048]{1,0:T(8,128)(2,1)}, bf16[224,2048]{1,0:T(8,128)(2,1)}, u32[]{:S(2)}, u32[]{:S(2)}) collective-permute-start(bf16[224,2048]{1,0:T(8,128)(2,1)} %get-tuple-element.20), channel_id=1, source_target_pairs={{0,8},{1,9},{2,10},{3,11},{4,12},{5,13},{6,14},{7,15},{8,16},{9,17... | collective-permute-start | bytes 2752520 | tf_op jit(solution)/shard_map/ppermute | solution.py:32
  81.0 26.3 %collective-permute-start.26 = (bf16[224,2048]{1,0:T(8,128)(2,1)}, bf16[224,2048]{1,0:T(8,128)(2,1)S(1)}, u32[]{:S(2)}, u32[]{:S(2)}) collective-permute-start(bf16[224,2048]{1,0:T(8,128)(2,1)} %get-tuple-element.20), channel_id=1, source_target_pairs={{8,0},{9,1},{10,2},{11,3},{12,4},{13,5},{14,6},{15,7},{16,8},{17,9... | collective-permute-start | bytes 2752520 | tf_op jit(solution)/shard_map/ppermute | solution.py:32
  84.5 29.3 %collective-permute-start.4 = (bf16[112,4096]{1,0:T(8,128)(2,1)}, bf16[112,4096]{1,0:T(8,128)(2,1)S(1)}, u32[]{:S(2)}, u32[]{:S(2)}) collective-permute-start(bf16[112,4096]{1,0:T(8,128)(2,1)} %copy-done.13), channel_id=1, source_target_pairs={{2,2},{3,10},{6,6},{7,14},{10,3},{11,11},{14,7},{15,15},{16,16},{1... | collective-permute-start | bytes 2752520 | tf_op jit(solution)/shard_map/ppermute | solution.py:32
  90.8 106.2 %collective-permute-start.7 = (bf16[4096,512]{1,0:T(8,128)(2,1)}, bf16[4096,512]{1,0:T(8,128)(2,1)}, u32[]{:S(2)}, u32[]{:S(2)}) collective-permute-start(bf16[4096,512]{1,0:T(8,128)(2,1)} %maximum_select_fusion), channel_id=1, source_target_pairs={{0,1},{1,0},{2,3},{3,2},{4,5},{5,4},{6,7},{7,6},{8,9},{9,8},{10,11... | collective-permute-start | bytes 12582920 | tf_op jit(solution)/shard_map/ppermute | solution.py:32
  110.4 31.0 %collective-permute-start.35 = (bf16[224,2048]{1,0:T(8,128)(2,1)}, bf16[224,2048]{1,0:T(8,128)(2,1)S(1)}, u32[]{:S(2)}, u32[]{:S(2)}) collective-permute-start(bf16[224,2048]{1,0:T(8,128)(2,1)} %get-tuple-element.18), channel_id=1, source_target_pairs={{0,4},{1,5},{2,6},{3,7},{4,0},{5,1},{6,2},{7,3},{8,12},{9,13},{10,... | collective-permute-start | bytes 2752520 | tf_op jit(solution)/shard_map/ppermute | solution.py:32
  112.5 27.6 %collective-permute-start.28 = (bf16[224,2048]{1,0:T(8,128)(2,1)}, bf16[224,2048]{1,0:T(8,128)(2,1)}, u32[]{:S(2)}, u32[]{:S(2)}) collective-permute-start(bf16[224,2048]{1,0:T(8,128)(2,1)} %copy-done.4), channel_id=1, source_target_pairs={{8,0},{9,1},{10,2},{11,3},{12,4},{13,5},{14,6},{15,7},{16,8},{17,9... | collective-permute-start | bytes 2752520 | tf_op jit(solution)/shard_map/ppermute | solution.py:32
  118.1 30.8 %collective-permute-start.37 = (bf16[448,1024]{1,0:T(8,128)(2,1)}, bf16[448,1024]{1,0:T(8,128)(2,1)}, u32[]{:S(2)}, u32[]{:S(2)}) collective-permute-start(bf16[448,1024]{1,0:T(8,128)(2,1)} %fusion.20), channel_id=1, source_target_pairs={{0,2},{4,6},{9,11},{13,15},{18,16},{22,20},{27,25},{31,29}} | collective-permute-start | bytes 2752520 | tf_op jit(solution)/shard_map/ppermute | solution.py:32
  120.4 31.2 %collective-permute-start.29 = (bf16[224,2048]{1,0:T(8,128)(2,1)}, bf16[224,2048]{1,0:T(8,128)(2,1)}, u32[]{:S(2)}, u32[]{:S(2)}) collective-permute-start(bf16[224,2048]{1,0:T(8,128)(2,1)} %collective-permute-done.27), channel_id=1, source_target_pairs={{16,24},{17,25},{18,26},{19,27},{20,28},{21,29},{22,30},{23,31}} | collective-permute-start | bytes 2752520 | tf_op jit(solution)/shard_map/ppermute | solution.py:32
  140.1 24.9 %collective-permute-start.30 = (bf16[224,2048]{1,0:T(8,128)(2,1)}, bf16[224,2048]{1,0:T(8,128)(2,1)}, u32[]{:S(2)}, u32[]{:S(2)}) collective-permute-start(bf16[224,2048]{1,0:T(8,128)(2,1)} %collective-permute-done.28), channel_id=1, source_target_pairs={{8,0},{9,1},{10,2},{11,3},{12,4},{13,5},{14,6},{15,7}} | collective-permute-start | bytes 2752520 | tf_op jit(solution)/shard_map/ppermute | solution.py:32
  145.4 22.9 %collective-permute-start.36 = (bf16[224,2048]{1,0:T(8,128)(2,1)}, bf16[224,2048]{1,0:T(8,128)(2,1)S(1)}, u32[]{:S(2)}, u32[]{:S(2)}) collective-permute-start(bf16[224,2048]{1,0:T(8,128)(2,1)} %get-tuple-element.16), channel_id=1, source_target_pairs={{0,4},{1,5},{2,6},{3,7},{4,0},{5,1},{6,2},{7,3},{8,12},{9,13},{10,... | collective-permute-start | bytes 2752520 | tf_op jit(solution)/shard_map/ppermute | solution.py:32
  149.0 22.0 %collective-permute-start.39 = (bf16[448,1024]{1,0:T(8,128)(2,1)}, bf16[448,1024]{1,0:T(8,128)(2,1)S(1)}, u32[]{:S(2)}, u32[]{:S(2)}) collective-permute-start(bf16[448,1024]{1,0:T(8,128)(2,1)} %fusion.19), channel_id=1, source_target_pairs={{0,2},{4,6},{9,11},{13,15},{18,16},{22,20},{27,25},{31,29}} | collective-permute-start | bytes 2752520 | tf_op jit(solution)/shard_map/ppermute | solution.py:32
  151.6 43.4 %collective-permute-start.8 = (bf16[4096,128]{1,0:T(8,128)(2,1)S(1)}, bf16[4096,128]{1,0:T(8,128)(2,1)S(1)}, u32[]{:S(2)}, u32[]{:S(2)}) collective-permute-start(bf16[4096,128]{1,0:T(8,128)(2,1)S(1)} %constant_dynamic-slice_fusion.3), channel_id=1, source_target_pairs={{0,1},{1,0},{2,3},{3,2},{4,5},{5,4},{6,7},{7,6},{8,9},{9,8},{10,11... | collective-permute-start | bytes 3145736 | tf_op jit(solution)/shard_map/ppermute | solution.py:32
  168.4 21.9 %collective-permute-start.31 = (bf16[224,2048]{1,0:T(8,128)(2,1)S(1)}, bf16[224,2048]{1,0:T(8,128)(2,1)S(1)}, u32[]{:S(2)}, u32[]{:S(2)}) collective-permute-start(bf16[224,2048]{1,0:T(8,128)(2,1)S(1)} %select_select_fusion.2), channel_id=1, source_target_pairs={{0,4},{1,5},{2,6},{3,7},{4,0},{5,1},{6,2},{7,3},{8,12},{9,13},{10,... | collective-permute-start | bytes 2752520 | tf_op jit(solution)/shard_map/ppermute | solution.py:32
  171.0 19.4 %collective-permute-start.41 = (bf16[448,1024]{1,0:T(8,128)(2,1)S(1)}, bf16[448,1024]{1,0:T(8,128)(2,1)S(1)}, u32[]{:S(2)}, u32[]{:S(2)}) collective-permute-start(bf16[448,1024]{1,0:T(8,128)(2,1)S(1)} %fusion.18), channel_id=1, source_target_pairs={{0,2},{4,6},{9,11},{13,15},{18,16},{22,20},{27,25},{31,29}} | collective-permute-start | bytes 2752520 | tf_op jit(solution)/shard_map/ppermute | solution.py:32
  172.6 20.0 %collective-permute-start.40 = (bf16[448,1024]{1,0:T(8,128)(2,1)S(1)}, bf16[448,1024]{1,0:T(8,128)(2,1)S(1)}, u32[]{:S(2)}, u32[]{:S(2)}) collective-permute-start(bf16[448,1024]{1,0:T(8,128)(2,1)S(1)} %broadcast_select_fusion.1), channel_id=1, source_target_pairs={{0,1},{2,3},{4,5},{6,7},{9,8},{11,10},{13,12},{15,14},{16,17},{18,... | collective-permute-start | bytes 2752520 | tf_op jit(solution)/shard_map/ppermute | solution.py:32
  190.2 23.2 %collective-permute-start.13 = (bf16[112,4096]{1,0:T(8,128)(2,1)S(1)}, bf16[112,4096]{1,0:T(8,128)(2,1)S(1)}, u32[]{:S(2)}, u32[]{:S(2)}) collective-permute-start(bf16[112,4096]{1,0:T(8,128)(2,1)S(1)} %copy-done.10), channel_id=1, source_target_pairs={{0,2},{1,3},{2,0},{3,1},{4,6},{5,7},{6,4},{7,5},{8,10},{9,11},{10,... | collective-permute-start | bytes 2752520 | tf_op jit(solution)/shard_map/ppermute | solution.py:32
  190.4 40.6 %collective-permute-start.5 = (bf16[112,4096]{1,0:T(8,128)(2,1)S(1)}, bf16[112,4096]{1,0:T(8,128)(2,1)S(1)}, u32[]{:S(2)}, u32[]{:S(2)}) collective-permute-start(bf16[112,4096]{1,0:T(8,128)(2,1)S(1)} %copy-done.12), channel_id=1, source_target_pairs={{0,2},{1,3},{2,0},{3,1},{4,6},{5,7},{6,4},{7,5},{8,10},{9,11},{10,... | collective-permute-start | bytes 2752520 | tf_op jit(solution)/shard_map/ppermute | solution.py:32
  192.6 53.5 %collective-permute-start.42 = (bf16[448,1024]{1,0:T(8,128)(2,1)S(1)}, bf16[448,1024]{1,0:T(8,128)(2,1)S(1)}, u32[]{:S(2)}, u32[]{:S(2)}) collective-permute-start(bf16[448,1024]{1,0:T(8,128)(2,1)S(1)} %broadcast_select_fusion), channel_id=1, source_target_pairs={{0,1},{2,3},{4,5},{6,7},{9,8},{11,10},{13,12},{15,14},{16,17},{18,... | collective-permute-start | bytes 2752520 | tf_op jit(solution)/shard_map/ppermute | solution.py:32
  195.0 43.5 %collective-permute-start.32 = (bf16[448,1024]{1,0:T(8,128)(2,1)S(1)}, bf16[448,1024]{1,0:T(8,128)(2,1)S(1)}, u32[]{:S(2)}, u32[]{:S(2)}) collective-permute-start(bf16[448,1024]{1,0:T(8,128)(2,1)S(1)} %fusion.21), channel_id=1, source_target_pairs={{0,2},{4,6},{9,11},{13,15},{18,16},{22,20},{27,25},{31,29}} | collective-permute-start | bytes 2752520 | tf_op jit(solution)/shard_map/ppermute | solution.py:32
  216.1 24.2 %collective-permute-start.15 = (bf16[224,640]{1,0:T(8,128)(2,1)S(1)}, bf16[224,640]{1,0:T(8,128)(2,1)S(1)}, u32[]{:S(2)}, u32[]{:S(2)}) collective-permute-start(bf16[224,640]{1,0:T(8,128)(2,1)S(1)} %get-tuple-element.28), channel_id=1, source_target_pairs={{0,17},{1,25},{2,19},{3,27},{4,21},{5,29},{6,23},{7,31},{8,16},{9,... | collective-permute-start | bytes 860168 | tf_op jit(solution)/shard_map/ppermute | solution.py:32
  216.4 26.2 %collective-permute-start.14 = (bf16[224,640]{1,0:T(8,128)(2,1)S(1)}, bf16[224,640]{1,0:T(8,128)(2,1)S(1)}, u32[]{:S(2)}, u32[]{:S(2)}) collective-permute-start(bf16[224,640]{1,0:T(8,128)(2,1)S(1)} %get-tuple-element.27), channel_id=1, source_target_pairs={{0,16},{1,24},{2,18},{3,26},{4,20},{5,28},{6,22},{7,30},{8,17},{9,... | collective-permute-start | bytes 860168 | tf_op jit(solution)/shard_map/ppermute | solution.py:32
  240.3 36.0 %collective-permute-start.33 = (bf16[448,1024]{1,0:T(8,128)(2,1)}, bf16[448,1024]{1,0:T(8,128)(2,1)}, u32[]{:S(2)}, u32[]{:S(2)}) collective-permute-start(bf16[448,1024]{1,0:T(8,128)(2,1)} %broadcast_select_fusion.3), channel_id=1, source_target_pairs={{0,1},{2,3},{4,5},{6,7},{9,8},{11,10},{13,12},{15,14},{16,17},{18,... | collective-permute-start | bytes 2752520 | tf_op jit(solution)/shard_map/ppermute | solution.py:32
  257.0 12.6 %collective-permute-start.22 = (f32[2,512]{1,0:T(2,128)S(1)}, f32[2,512]{1,0:T(2,128)S(1)}, u32[]{:S(2)}, u32[]{:S(2)}) collective-permute-start(f32[2,512]{1,0:T(2,128)S(1)} %fusion.52), channel_id=1, source_target_pairs={{0,16},{4,20},{8,24},{12,28},{16,0},{20,4},{24,8},{28,12},{1,17},{... | collective-permute-start | bytes 12296 | tf_op jit(solution)/shard_map/ppermute | solution.py:20
  (29 other events, 378.4 us)
where the time goes:
time: 285 us; the launch traced here: 284 us
  waiting for transfers between devices  133 us (47%)
  starting transfers between devices  69.1 us (24%)
  other arithmetic  41.7 us (15%)
  matrix products  22.2 us (8%)
  local copies, waits for them, and re-layouts  9.52 us (3%)
  between operations  7.91 us (3%)
    ppermute x34, waiting for transfers between devices, send(): return lax.ppermute(value, ('dp', 'head'), pairs)  111 us
    ppermute x34, starting transfers between devices, send(): return lax.ppermute(value, ('dp', 'head'), pairs)  59.1 us
    ppermute x9, waiting for transfers between devices, partner_2(): return lax.ppermute(value, axis, pairs)  21.9 us
    dot_general x2, matrix products, dot(): lax.dot_general(jnp.concatenate(parts_a), jnp.concatenate(parts_b), (((0,...  16.4 us
    ppermute x9, starting transfers between devices, partner_2(): return lax.ppermute(value, axis, pairs)  10 us
    unnamed x3, other arithmetic  8.03 us
  transfers between devices with their start and end apart: 43, of which 16 were waited for; matrix products, arithmetic and copies ran while one was open for 23% of the time, Pallas kernels for 0%

commit v1 on v0

--- a/solution.py
+++ b/solution.py
@@ -176,12 +176,18 @@
             return 2 * (2 * ((z // 2) ^ e) + c) + y, 2 * x + z % 2
 
         def kept(d, h, e=e, to_plane=to_plane):
-            return to_plane(d, h) if ((d // 4) ^ e) == h // 2 else None
+            moves = to_plane(d, h) != (d, h) and ((d // 4) ^ e) == h // 2
+            return to_plane(d, h) if moves else None
 
         def passed(d, h, e=e, to_plane=to_plane):
-            return to_plane(d, h) if ((d // 4) ^ e) != h // 2 else None
-
-        mine = jnp.where(w == x, send(keep, kept), send(came, passed))
+            moves = to_plane(d, h) != (d, h) and ((d // 4) ^ e) != h // 2
+            return to_plane(d, h) if moves else None
+
+        sent_keep, sent_came = send(keep, kept), send(came, passed)
+        if e == 0:
+            sent_keep = jnp.where(p == c, keep, sent_keep)
+            sent_came = jnp.where(p == c, came, sent_came)
+        mine = jnp.where(w == x, sent_keep, sent_came)
         tokens = jnp.concatenate([mine, flip_x(mine)])
         product = jnp.dot(tokens, matrix, preferred_element_type=jnp.float32)
         product = product.astype(jnp.bfloat16)
@@ -192,7 +198,13 @@
                 z, y, x, c = d // 2, d % 2, h // 2, h % 2
                 return 2 * (2 * ((z // 2) ^ e) + c) + y, 2 * x + ((z % 2) ^ f)
 
-            part = send(chunk, to_group).astype(jnp.float32)
+            def moved(d, h, to_group=to_group):
+                return to_group(d, h) if to_group(d, h) != (d, h) else None
+
+            part = send(chunk, moved)
+            if e == 0 and f == 0:
+                part = jnp.where(p == c, chunk, part)
+            part = part.astype(jnp.float32)
             total = part if total is None else total + part
     return total
 
@@ -244,7 +256,7 @@
             block = arrival(up, down, tie(z, block), step)
         pair = jnp.concatenate([block, flip_y(block)])
         cut = lax.dynamic_slice_in_dim(pair, y * col_span, col_span, 1)
-        if step == last:
+        if step == last - 1:
             early = dot(row_parts, col_parts)
             early = lax.optimization_barrier(early)
         across = send(cut, lambda d, h: (d, h ^ 2) if h == d // 2 else None)
@@ -252,7 +264,7 @@
         twin = send(have, lambda d, h: (d, h ^ 1) if h in (d // 2, (d // 2) ^ 2) else None)
         row_parts.append(pair)
         col_parts.append(jnp.where((h == z) | (h == (z ^ 2)), have, twin))
-    return (dot(row_parts[-1:], col_parts[-1:]) + early) / counted
+    return (dot(row_parts[-2:], col_parts[-2:]) + early) / counted
 
 
 def planes(hidden, norm_gain, query_weight, kv_weight, own_lengths, length_max, counted):
@@ -262,7 +274,10 @@
     slot_count = rows // length_max
     span = cols // 2
     sequences = hidden.reshape(slot_count, length_max, cols)
-    raw = flip_x(take(sequences, 1 - x))
+    first, second = hidden[:, :span], hidden[:, span:]
+    near = send(jnp.where(h == 0, second, first), lambda d, h: (d, h + 1) if h < 2 else None)
+    far = send(second, lambda d, h: (d, 3) if h == 1 else None)
+    raw = flip_x(take(sequences, 1 - tie(x, (near, far))))
     other_rows = flip_y(query_weight)
     widened = hidden.astype(jnp.float32)
     local = jnp.sum(widened * widened, axis=1)
@@ -274,10 +289,6 @@
     came = scale_by(
         raw, tie(slot_factor, keep), lax.dynamic_slice_in_dim(norm_gain, (h ^ 2) * cols, cols)
     )
-    first, second = hidden[:, :span], hidden[:, span:]
-    late = tie(h, raw)
-    near = send(jnp.where(late == 0, second, first), lambda d, h: (d, h + 1) if h < 2 else None)
-    far = send(jnp.where(late == 1, second, first), lambda d, h: (d, 3) if h == 1 else None)
     total = project_planes(keep, came, query_weight, other_rows, kv_weight)
     block = scale_by(
         jnp.where(h == 0, first, jnp.where(h == 3, far, near)),

time: 285 us -> 282 us (0.989)
  waiting for transfers between devices: 133 us -> 98.4 us
  starting transfers between devices: 69.1 us -> 94.9 us
  matrix products: 22.2 us -> 28.4 us
    ppermute x34, starting transfers between devices: 59.1 us -> 91.3 us  [send(): return lax.ppermute(value, ('dp', 'head'), pairs)]
    ppermute x34, waiting for transfers between devices: 111 us -> 84.5 us  [send(): return lax.ppermute(value, ('dp', 'head'), pairs)]
    unnamed x3 -> x0, other arithmetic: 8.03 us -> none
    ppermute x9, waiting for transfers between devices: 21.9 us -> 13.9 us  [partner_2(): return lax.ppermute(value, axis, pairs)]
    ppermute x9, starting transfers between devices: 10 us -> 3.67 us  [partner_2(): return lax.ppermute(value, axis, pairs)]
    convert_element_type x2 -> x3, other arithmetic: 1.53 us -> 6.37 us  [scale_by(): (values.astype(jnp.float32) * factor[:, None] * gain[None, :]).astype(jnp...]
    select_n x1 -> x3, other arithmetic: 1.37 us -> 5.46 us  [arrival(): block = mine if block is None else jnp.where(z == plane, mine, block)]
    dot_general x2, matrix products: 16.4 us -> 19.8 us  [dot(): lax.dot_general(jnp.concatenate(parts_a), jnp.concatenate(parts_b), (((0,...]
  transfers between devices with their start and end apart: 43 -> 43, of which waited for: 16 -> 17; matrix products, arithmetic and copies ran while one was open for 23% -> 25% of each run, Pallas kernels for 0% -> 0%
where the time goes in v1:
time: 282 us; the launch traced here: 281 us
  waiting for transfers between devices  98.4 us (35%)
  starting transfers between devices  94.9 us (34%)
  other arithmetic  43 us (15%)
  matrix products  28.4 us (10%)
  local copies, waits for them, and re-layouts  8.63 us (3%)
  between operations  7.62 us (3%)
    ppermute x34, starting transfers between devices, send(): return lax.ppermute(value, ('dp', 'head'), pairs)  91.3 us
    ppermute x34, waiting for transfers between devices, send(): return lax.ppermute(value, ('dp', 'head'), pairs)  84.5 us
    dot_general x2, matrix products, dot(): lax.dot_general(jnp.concatenate(parts_a), jnp.concatenate(parts_b), (((0,...  19.8 us
    ppermute x9, waiting for transfers between devices, partner_2(): return lax.ppermute(value, axis, pairs)  13.9 us
    convert_element_type x3, other arithmetic, scale_by(): (values.astype(jnp.float32) * factor[:, None] * gain[None, :]).astype(jnp...  6.37 us
  transfers between devices with their start and end apart: 43, of which 17 were waited for; matrix products, arithmetic and copies ran while one was open for 25% of the time, Pallas kernels for 0%

profile of v1, /device:TPU:0, one launch (start us, length us, event | category | flops | bytes accessed | tf_op | source)
XLA Modules:
  0.0 281.0 jit_solution(5870172587836559693)
XLA Ops:
  0.7 3.1 %collective-permute-start.8 = (bf16[2048,512]{1,0:T(8,128)(2,1)}, bf16[2048,512]{1,0:T(8,128)(2,1)}, u32[]{:S(2)}, u32[]{:S(2)}) collective-permute-start(bf16[2048,512]{1,0:T(8,128)(2,1)} %param.8), channel_id=1, source_target_pairs={{0,4},{1,5},{2,6},{3,7},{4,0},{5,1},{6,2},{7,3},{8,12},{9,13},{10,... | collective-permute-start | bytes 6291464 | tf_op jit(solution)/shard_map/ppermute | solution.py:32
  5.8 2.8 %fusion.57 = (bf16[224,2048]{1,0:T(8,128)(2,1)}, bf16[224,2048]{1,0:T(8,128)(2,1)}) fusion(bf16[224,4096]{1,0:T(8,128)(2,1)} %param.6, pred[]{:T(512)S(6)} %eq.84), kind=kLoop, calls=%fused_computation.134 | loop fusion | flops 458752 | bytes 3670017 | tf_op jit(solution)/shard_map/slice | solution.py:277
  8.6 3.4 %collective-permute-start.3 = (bf16[224,2048]{1,0:T(8,128)(2,1)}, bf16[224,2048]{1,0:T(8,128)(2,1)}, u32[]{:S(2)}, u32[]{:S(2)}) collective-permute-start(bf16[224,2048]{1,0:T(8,128)(2,1)} %get-tuple-element.16), channel_id=1, source_target_pairs={{0,1},{1,2},{4,5},{5,6},{8,9},{9,10},{12,13},{13,14},{16,17},{17,1... | collective-permute-start | bytes 2752520 | tf_op jit(solution)/shard_map/ppermute | solution.py:32
  25.6 2.7 multiply_convert_fusion
  28.2 4.4 %collective-permute-start.25 = (bf16[224,2048]{1,0:T(8,128)(2,1)}, bf16[224,2048]{1,0:T(8,128)(2,1)}, u32[]{:S(2)}, u32[]{:S(2)}) collective-permute-start(bf16[224,2048]{1,0:T(8,128)(2,1)} %multiply_convert_fusion), channel_id=1, source_target_pairs={{0,8},{1,9},{2,10},{3,11},{4,12},{5,13},{6,14},{7,15},{8,16},{9,17... | collective-permute-start | bytes 2752520 | tf_op jit(solution)/shard_map/ppermute | solution.py:32
  39.0 7.6 %collective-permute-done.25 = bf16[224,2048]{1,0:T(8,128)(2,1)} collective-permute-done((bf16[224,2048]{1,0:T(8,128)(2,1)}, bf16[224,2048]{1,0:T(8,128)(2,1)}, u32[]{:S(2)}, u32[]{:S(2)}) %collective-permute-start.25) | collective-permute-done | bytes 917536 | tf_op jit(solution)/shard_map/ppermute | solution.py:32
  47.1 5.1 %collective-permute-done.26 = bf16[224,2048]{1,0:T(8,128)(2,1)} collective-permute-done((bf16[224,2048]{1,0:T(8,128)(2,1)}, bf16[224,2048]{1,0:T(8,128)(2,1)}, u32[]{:S(2)}, u32[]{:S(2)}) %collective-permute-start.26) | collective-permute-done | bytes 917536 | tf_op jit(solution)/shard_map/ppermute | solution.py:32
  52.1 2.5 select_select_fusion.1
  59.2 5.5 %collective-permute-done.37 = bf16[224,2048]{1,0:T(8,128)(2,1)} collective-permute-done((bf16[224,2048]{1,0:T(8,128)(2,1)}, bf16[224,2048]{1,0:T(8,128)(2,1)}, u32[]{:S(2)}, u32[]{:S(2)}) %collective-permute-start.37) | collective-permute-done | bytes 917536 | tf_op jit(solution)/shard_map/ppermute | solution.py:32
  69.6 4.2 %maximum_select_fusion = bf16[4096,512]{1,0:T(8,128)(2,1)} fusion(bf16[2048,512]{1,0:T(8,128)(2,1)} %collective-permute-done.8, bf16[2048,512]{1,0:T(8,128)(2,1)S(1)} %copy-done.5, pred[]{:T(512)S(6)} %eq.85), kind=kLoop, calls=%fused_computation.2 | loop fusion | flops 18874368 | bytes 8388609 | tf_op jit(solution)/shard_map/jit(_where)/select_n | solution.py:162
  73.8 10.6 %collective-permute-done.38 = bf16[224,2048]{1,0:T(8,128)(2,1)} collective-permute-done((bf16[224,2048]{1,0:T(8,128)(2,1)}, bf16[224,2048]{1,0:T(8,128)(2,1)}, u32[]{:S(2)}, u32[]{:S(2)}) %collective-permute-start.38) | collective-permute-done | bytes 917536 | tf_op jit(solution)/shard_map/ppermute | solution.py:32
  87.0 6.1 %collective-permute-start.39 = (bf16[448,1024]{1,0:T(8,128)(2,1)S(1)}, bf16[448,1024]{1,0:T(8,128)(2,1)S(1)}, u32[]{:S(2)}, u32[]{:S(2)}) collective-permute-start(bf16[448,1024]{1,0:T(8,128)(2,1)S(1)} %fusion.34), channel_id=1, source_target_pairs={{0,2},{4,6},{9,11},{13,15},{18,16},{22,20},{27,25},{31,29}} | collective-permute-start | bytes 2752520 | tf_op jit(solution)/shard_map/ppermute | solution.py:32
  97.3 3.0 %select_select_fusion.3 = bf16[112,4096]{1,0:T(8,128)(2,1)} fusion(bf16[112,4096]{1,0:T(8,128)(2,1)} %collective-permute-done.6, bf16[112,4096]{1,0:T(8,128)(2,1)} %collective-permute-done.2, pred[]{:T(512)S(6)} %eq.82, pred[]{:T(512)S(6)} %eq.83, f32[4096]{0:T(1024)S(1)} %get-tuple-element.27, f32[112]{0:T(128)S(1)} %fusion.49, ...), kind=kLoop, calls=%fused_computation.58 | loop fusion | flops 5046272 | bytes 4621318 | tf_op jit(solution)/shard_map/jit(_where)/select_n | solution.py:190
  103.9 7.1 %collective-permute-start.14 = (bf16[112,4096]{1,0:T(8,128)(2,1)}, bf16[112,4096]{1,0:T(8,128)(2,1)}, u32[]{:S(2)}, u32[]{:S(2)}) collective-permute-start(bf16[112,4096]{1,0:T(8,128)(2,1)} %multiply_convert_fusion.1), channel_id=1, source_target_pairs={{0,16},{1,24},{4,20},{5,28},{8,17},{9,25},{12,21},{13,29},{18,2},{... | collective-permute-start | bytes 2752520 | tf_op jit(solution)/shard_map/ppermute | solution.py:32
  111.0 2.7 collective-permute-done.41
  117.0 2.5 collective-permute-start.29
  121.0 18.2 %collective-permute-start.40 = (bf16[448,1024]{1,0:T(8,128)(2,1)}, bf16[448,1024]{1,0:T(8,128)(2,1)S(1)}, u32[]{:S(2)}, u32[]{:S(2)}) collective-permute-start(bf16[448,1024]{1,0:T(8,128)(2,1)} %broadcast_select_fusion.1), channel_id=1, source_target_pairs={{0,1},{2,3},{4,5},{6,7},{9,8},{11,10},{13,12},{15,14},{16,17},{18,... | collective-permute-start | bytes 2752520 | tf_op jit(solution)/shard_map/ppermute | solution.py:32
  144.2 11.1 %collective-permute-start.15 = (bf16[112,4096]{1,0:T(8,128)(2,1)S(1)}, bf16[112,4096]{1,0:T(8,128)(2,1)S(1)}, u32[]{:S(2)}, u32[]{:S(2)}) collective-permute-start(bf16[112,4096]{1,0:T(8,128)(2,1)S(1)} %broadcast_select_fusion.9), channel_id=1, source_target_pairs={{0,2},{1,3},{2,0},{3,1},{4,6},{5,7},{6,4},{7,5},{8,10},{9,11},{10,... | collective-permute-start | bytes 2752520 | tf_op jit(solution)/shard_map/ppermute | solution.py:32
  155.4 8.3 %collective-permute-done.32 = bf16[224,2048]{1,0:T(8,128)(2,1)S(1)} collective-permute-done((bf16[224,2048]{1,0:T(8,128)(2,1)S(1)}, bf16[224,2048]{1,0:T(8,128)(2,1)S(1)}, u32[]{:S(2)}, u32[]{:S(2)}) %collective-permute-start.32) | collective-permute-done | bytes 917536 | tf_op jit(solution)/shard_map/ppermute | solution.py:32
  163.7 3.4 %collective-permute-start.33 = (bf16[448,1024]{1,0:T(8,128)(2,1)S(1)}, bf16[448,1024]{1,0:T(8,128)(2,1)S(1)}, u32[]{:S(2)}, u32[]{:S(2)}) collective-permute-start(bf16[448,1024]{1,0:T(8,128)(2,1)S(1)} %fusion.36), channel_id=1, source_target_pairs={{0,2},{4,6},{9,11},{13,15},{18,16},{22,20},{27,25},{31,29}} | collective-permute-start | bytes 2752520 | tf_op jit(solution)/shard_map/ppermute | solution.py:32
  168.9 10.1 %fusion.7 = f32[2048,1024]{1,0:T(8,128)} fusion(bf16[224,2048]{1,0:T(8,128)(2,1)} %collective-permute-done.38, bf16[224,2048]{1,0:T(8,128)(2,1)} %select_select_fusion.1, bf16[224,2048]{1,0:T(8,128)(2,1)} %collective-permute-done.37, bf16[224,2048]{1,0:T(8,128)(2,1)} %multiply_convert_fusion, bf16[448,1024]{1,0:T(8,128)(2,1)S(1)} %broadcast_select_fusion.4, ...), kind=kOutput, calls=%fused_computation.10 | convolution fusion | flops 3776446464 | bytes 13893632 | tf_op jit(solution)/shard_map/dot_general | solution.py:246
  178.9 16.3 %collective-permute-done.33 = bf16[448,1024]{1,0:T(8,128)(2,1)S(1)} collective-permute-done((bf16[448,1024]{1,0:T(8,128)(2,1)S(1)}, bf16[448,1024]{1,0:T(8,128)(2,1)S(1)}, u32[]{:S(2)}, u32[]{:S(2)}) %collective-permute-start.33) | collective-permute-done | bytes 917536 | tf_op jit(solution)/shard_map/ppermute | solution.py:32
  197.8 7.2 %collective-permute-done.35 = bf16[448,1024]{1,0:T(8,128)(2,1)S(1)} collective-permute-done((bf16[448,1024]{1,0:T(8,128)(2,1)S(1)}, bf16[448,1024]{1,0:T(8,128)(2,1)S(1)}, u32[]{:S(2)}, u32[]{:S(2)}) %collective-permute-start.35) | collective-permute-done | bytes 917536 | tf_op jit(solution)/shard_map/ppermute | solution.py:32
  207.9 5.0 %pad_maximum_fusion = bf16[4096,1280]{1,0:T(8,128)(2,1)S(1)} fusion(bf16[4096,128]{1,0:T(8,128)(2,1)S(1)} %collective-permute-done.10, bf16[4096,512]{1,0:T(8,128)(2,1)} %collective-permute-done.9, bf16[4096,128]{1,0:T(8,128)(2,1)S(1)} %constant_dynamic-slice_fusion.3, bf16[4096,512]{1,0:T(8,128)(2,1)} %maximum_select_fusion), kind=kLoop, calls=%fused_computation | loop fusion | flops 41943040 | bytes 20971520 | tf_op jit(solution)/shard_map/concatenate | solution.py:168
  212.9 2.6 convolution_convert_fusion
  215.6 4.5 %collective-permute-start.16 = (bf16[224,640]{1,0:T(8,128)(2,1)S(1)}, bf16[224,640]{1,0:T(8,128)(2,1)S(1)}, u32[]{:S(2)}, u32[]{:S(2)}) collective-permute-start(bf16[224,640]{1,0:T(8,128)(2,1)S(1)} %get-tuple-element.21), channel_id=1, source_target_pairs={{0,16},{1,24},{2,18},{3,26},{4,20},{5,28},{6,22},{7,30},{8,17},{9,... | collective-permute-start | bytes 860168 | tf_op jit(solution)/shard_map/ppermute | solution.py:32
  220.1 2.6 convolution_convert_fusion.1
  226.0 17.3 %collective-permute-done.16 = bf16[224,640]{1,0:T(8,128)(2,1)S(1)} collective-permute-done((bf16[224,640]{1,0:T(8,128)(2,1)S(1)}, bf16[224,640]{1,0:T(8,128)(2,1)S(1)}, u32[]{:S(2)}, u32[]{:S(2)}) %collective-permute-start.16) | collective-permute-done | bytes 286752 | tf_op jit(solution)/shard_map/ppermute | solution.py:32
  253.8 3.2 %collective-permute-done.22 = f32[2,512]{1,0:T(2,128)S(1)} collective-permute-done((f32[2,512]{1,0:T(2,128)S(1)}, f32[2,512]{1,0:T(2,128)S(1)}, u32[]{:S(2)}, u32[]{:S(2)}) %collective-permute-start.22) | collective-permute-done | bytes 4128 | tf_op jit(solution)/shard_map/ppermute | solution.py:20
  257.6 3.1 %collective-permute-done.23 = f32[2,512]{1,0:T(2,128)S(1)} collective-permute-done((f32[2,512]{1,0:T(2,128)S(1)}, f32[2,512]{1,0:T(2,128)S(1)}, u32[]{:S(2)}, u32[]{:S(2)}) %collective-permute-start.23) | collective-permute-done | bytes 4128 | tf_op jit(solution)/shard_map/ppermute | solution.py:20
  264.1 9.7 %add_divide_fusion = f32[2048,1024]{1,0:T(8,128)} fusion(f32[2048,1024]{1,0:T(8,128)} %fusion.7, f32[]{:T(128)S(6)} %convert_element_type.108, bf16[224,2048]{1,0:T(8,128)(2,1)} %copy-done.9, bf16[224,2048]{1,0:T(8,128)(2,1)S(1)} %copy-done.4, bf16[224,2048]{1,0:T(8,128)(2,1)S(1)} %copy-done.8, bf16[224,2048]{1,0:T(8,128)(2,1)S(1)} %fusion.32, ...), kind=kOutput, calls=%fused_computation.1 | convolution fusion | flops 3780640768 | bytes 22282244 | tf_op jit(solution)/shard_map/dot_general | solution.py:246
  274.6 5.7 %collective-permute-done.21 = bf16[112,512]{1,0:T(8,128)(2,1)S(1)} collective-permute-done((bf16[112,512]{1,0:T(8,128)(2,1)S(1)}, bf16[112,512]{1,0:T(8,128)(2,1)S(1)}, u32[]{:S(2)}, u32[]{:S(2)}) %collective-permute-start.21) | collective-permute-done | bytes 114720 | tf_op jit(solution)/shard_map/ppermute | solution.py:20
  (166 shorter events, 71.9 us)
Async XLA Ops:
  0.7 65.7 %collective-permute-start.8 = (bf16[2048,512]{1,0:T(8,128)(2,1)}, bf16[2048,512]{1,0:T(8,128)(2,1)}, u32[]{:S(2)}, u32[]{:S(2)}) collective-permute-start(bf16[2048,512]{1,0:T(8,128)(2,1)} %param.8), channel_id=1, source_target_pairs={{0,4},{1,5},{2,6},{3,7},{4,0},{5,1},{6,2},{7,3},{8,12},{9,13},{10,... | collective-permute-start | bytes 6291464 | tf_op jit(solution)/shard_map/ppermute | solution.py:32
  8.6 16.9 %collective-permute-start.3 = (bf16[224,2048]{1,0:T(8,128)(2,1)}, bf16[224,2048]{1,0:T(8,128)(2,1)}, u32[]{:S(2)}, u32[]{:S(2)}) collective-permute-start(bf16[224,2048]{1,0:T(8,128)(2,1)} %get-tuple-element.16), channel_id=1, source_target_pairs={{0,1},{1,2},{4,5},{5,6},{8,9},{9,10},{12,13},{13,14},{16,17},{17,1... | collective-permute-start | bytes 2752520 | tf_op jit(solution)/shard_map/ppermute | solution.py:32
  28.2 18.3 %collective-permute-start.25 = (bf16[224,2048]{1,0:T(8,128)(2,1)}, bf16[224,2048]{1,0:T(8,128)(2,1)}, u32[]{:S(2)}, u32[]{:S(2)}) collective-permute-start(bf16[224,2048]{1,0:T(8,128)(2,1)} %multiply_convert_fusion), channel_id=1, source_target_pairs={{0,8},{1,9},{2,10},{3,11},{4,12},{5,13},{6,14},{7,15},{8,16},{9,17... | collective-permute-start | bytes 2752520 | tf_op jit(solution)/shard_map/ppermute | solution.py:32
  32.6 19.5 %collective-permute-start.26 = (bf16[224,2048]{1,0:T(8,128)(2,1)}, bf16[224,2048]{1,0:T(8,128)(2,1)}, u32[]{:S(2)}, u32[]{:S(2)}) collective-permute-start(bf16[224,2048]{1,0:T(8,128)(2,1)} %multiply_convert_fusion), channel_id=1, source_target_pairs={{8,0},{9,1},{10,2},{11,3},{12,4},{13,5},{14,6},{15,7},{16,8},{17,9... | collective-permute-start | bytes 2752520 | tf_op jit(solution)/shard_map/ppermute | solution.py:32
  35.0 20.1 %collective-permute-start.5 = (bf16[112,4096]{1,0:T(8,128)(2,1)}, bf16[112,4096]{1,0:T(8,128)(2,1)}, u32[]{:S(2)}, u32[]{:S(2)}) collective-permute-start(bf16[112,4096]{1,0:T(8,128)(2,1)} %dynamic-slice_bitcast_fusion), channel_id=1, source_target_pairs={{0,2},{1,3},{2,0},{3,1},{4,6},{5,7},{6,4},{7,5},{8,10},{9,11},{10,... | collective-permute-start | bytes 2752520 | tf_op jit(solution)/shard_map/ppermute | solution.py:32
  37.3 49.6 %collective-permute-start.2 = (bf16[112,4096]{1,0:T(8,128)(2,1)}, bf16[112,4096]{1,0:T(8,128)(2,1)}, u32[]{:S(2)}, u32[]{:S(2)}) collective-permute-start(bf16[112,4096]{1,0:T(8,128)(2,1)} %fusion.28), channel_id=1, source_target_pairs={{1,8},{5,12},{8,1},{12,5},{19,26},{23,30},{26,19},{30,23}} | collective-permute-start | bytes 2752520 | tf_op jit(solution)/shard_map/ppermute | solution.py:32
  46.6 18.2 %collective-permute-start.37 = (bf16[224,2048]{1,0:T(8,128)(2,1)}, bf16[224,2048]{1,0:T(8,128)(2,1)}, u32[]{:S(2)}, u32[]{:S(2)}) collective-permute-start(bf16[224,2048]{1,0:T(8,128)(2,1)} %multiply_convert_fusion), channel_id=1, source_target_pairs={{0,4},{1,5},{2,6},{3,7},{4,0},{5,1},{6,2},{7,3},{8,12},{9,13},{10,... | collective-permute-start | bytes 2752520 | tf_op jit(solution)/shard_map/ppermute | solution.py:32
  54.6 29.8 %collective-permute-start.38 = (bf16[224,2048]{1,0:T(8,128)(2,1)}, bf16[224,2048]{1,0:T(8,128)(2,1)}, u32[]{:S(2)}, u32[]{:S(2)}) collective-permute-start(bf16[224,2048]{1,0:T(8,128)(2,1)} %select_select_fusion.1), channel_id=1, source_target_pairs={{0,4},{1,5},{2,6},{3,7},{4,0},{5,1},{6,2},{7,3},{8,12},{9,13},{10,... | collective-permute-start | bytes 2752520 | tf_op jit(solution)/shard_map/ppermute | solution.py:32
  57.6 35.4 %collective-permute-start.6 = (bf16[112,4096]{1,0:T(8,128)(2,1)}, bf16[112,4096]{1,0:T(8,128)(2,1)}, u32[]{:S(2)}, u32[]{:S(2)}) collective-permute-start(bf16[112,4096]{1,0:T(8,128)(2,1)} %multiply_convert_fusion.1), channel_id=1, source_target_pairs={{3,10},{7,14},{10,3},{14,7},{17,24},{21,28},{24,17},{28,21}} | collective-permute-start | bytes 2752520 | tf_op jit(solution)/shard_map/ppermute | solution.py:32
  64.8 29.7 %collective-permute-start.27 = (bf16[224,2048]{1,0:T(8,128)(2,1)}, bf16[224,2048]{1,0:T(8,128)(2,1)}, u32[]{:S(2)}, u32[]{:S(2)}) collective-permute-start(bf16[224,2048]{1,0:T(8,128)(2,1)} %collective-permute-done.25), channel_id=1, source_target_pairs={{8,16},{9,17},{10,18},{11,19},{12,20},{13,21},{14,22},{15,23},{16,... | collective-permute-start | bytes 2752520 | tf_op jit(solution)/shard_map/ppermute | solution.py:32
  66.4 29.7 %collective-permute-start.28 = (bf16[224,2048]{1,0:T(8,128)(2,1)}, bf16[224,2048]{1,0:T(8,128)(2,1)}, u32[]{:S(2)}, u32[]{:S(2)}) collective-permute-start(bf16[224,2048]{1,0:T(8,128)(2,1)} %collective-permute-done.26), channel_id=1, source_target_pairs={{8,0},{9,1},{10,2},{11,3},{12,4},{13,5},{14,6},{15,7},{16,8},{17,9... | collective-permute-start | bytes 2752520 | tf_op jit(solution)/shard_map/ppermute | solution.py:32
  84.4 56.2 %collective-permute-start.13 = (bf16[112,4096]{1,0:T(8,128)(2,1)}, bf16[112,4096]{1,0:T(8,128)(2,1)}, u32[]{:S(2)}, u32[]{:S(2)}) collective-permute-start(bf16[112,4096]{1,0:T(8,128)(2,1)} %fusion.28), channel_id=1, source_target_pairs={{2,18},{3,26},{6,22},{7,30},{10,19},{11,27},{14,23},{15,31},{16,0}... | collective-permute-start | bytes 2752520 | tf_op jit(solution)/shard_map/ppermute | solution.py:32
  87.0 16.9 %collective-permute-start.39 = (bf16[448,1024]{1,0:T(8,128)(2,1)S(1)}, bf16[448,1024]{1,0:T(8,128)(2,1)S(1)}, u32[]{:S(2)}, u32[]{:S(2)}) collective-permute-start(bf16[448,1024]{1,0:T(8,128)(2,1)S(1)} %fusion.34), channel_id=1, source_target_pairs={{0,2},{4,6},{9,11},{13,15},{18,16},{22,20},{27,25},{31,29}} | collective-permute-start | bytes 2752520 | tf_op jit(solution)/shard_map/ppermute | solution.py:32
  93.1 20.7 %collective-permute-start.41 = (bf16[448,1024]{1,0:T(8,128)(2,1)S(1)}, bf16[448,1024]{1,0:T(8,128)(2,1)S(1)}, u32[]{:S(2)}, u32[]{:S(2)}) collective-permute-start(bf16[448,1024]{1,0:T(8,128)(2,1)S(1)} %fusion.33), channel_id=1, source_target_pairs={{0,2},{4,6},{9,11},{13,15},{18,16},{22,20},{27,25},{31,29}} | collective-permute-start | bytes 2752520 | tf_op jit(solution)/shard_map/ppermute | solution.py:32
  94.4 22.6 %collective-permute-start.30 = (bf16[224,2048]{1,0:T(8,128)(2,1)}, bf16[224,2048]{1,0:T(8,128)(2,1)}, u32[]{:S(2)}, u32[]{:S(2)}) collective-permute-start(bf16[224,2048]{1,0:T(8,128)(2,1)} %collective-permute-done.27), channel_id=1, source_target_pairs={{16,24},{17,25},{18,26},{19,27},{20,28},{21,29},{22,30},{23,31}} | collective-permute-start | bytes 2752520 | tf_op jit(solution)/shard_map/ppermute | solution.py:32
  96.0 25.0 %collective-permute-start.31 = (bf16[224,2048]{1,0:T(8,128)(2,1)}, bf16[224,2048]{1,0:T(8,128)(2,1)}, u32[]{:S(2)}, u32[]{:S(2)}) collective-permute-start(bf16[224,2048]{1,0:T(8,128)(2,1)} %collective-permute-done.28), channel_id=1, source_target_pairs={{8,0},{9,1},{10,2},{11,3},{12,4},{13,5},{14,6},{15,7}} | collective-permute-start | bytes 2752520 | tf_op jit(solution)/shard_map/ppermute | solution.py:32
  103.9 38.2 %collective-permute-start.14 = (bf16[112,4096]{1,0:T(8,128)(2,1)}, bf16[112,4096]{1,0:T(8,128)(2,1)}, u32[]{:S(2)}, u32[]{:S(2)}) collective-permute-start(bf16[112,4096]{1,0:T(8,128)(2,1)} %multiply_convert_fusion.1), channel_id=1, source_target_pairs={{0,16},{1,24},{4,20},{5,28},{8,17},{9,25},{12,21},{13,29},{18,2},{... | collective-permute-start | bytes 2752520 | tf_op jit(solution)/shard_map/ppermute | solution.py:32
  114.7 93.2 %collective-permute-start.9 = (bf16[4096,512]{1,0:T(8,128)(2,1)}, bf16[4096,512]{1,0:T(8,128)(2,1)}, u32[]{:S(2)}, u32[]{:S(2)}) collective-permute-start(bf16[4096,512]{1,0:T(8,128)(2,1)} %maximum_select_fusion), channel_id=1, source_target_pairs={{0,1},{1,0},{2,3},{3,2},{4,5},{5,4},{6,7},{7,6},{8,9},{9,8},{10,11... | collective-permute-start | bytes 12582920 | tf_op jit(solution)/shard_map/ppermute | solution.py:32
  117.0 27.0 %collective-permute-start.29 = (bf16[224,2048]{1,0:T(8,128)(2,1)S(1)}, bf16[224,2048]{1,0:T(8,128)(2,1)S(1)}, u32[]{:S(2)}, u32[]{:S(2)}) collective-permute-start(bf16[224,2048]{1,0:T(8,128)(2,1)S(1)} %fusion.32), channel_id=1, source_target_pairs={{0,4},{1,5},{2,6},{3,7},{4,0},{5,1},{6,2},{7,3},{8,12},{9,13},{10,... | collective-permute-start | bytes 2752520 | tf_op jit(solution)/shard_map/ppermute | solution.py:32
  121.0 23.2 %collective-permute-start.40 = (bf16[448,1024]{1,0:T(8,128)(2,1)}, bf16[448,1024]{1,0:T(8,128)(2,1)S(1)}, u32[]{:S(2)}, u32[]{:S(2)}) collective-permute-start(bf16[448,1024]{1,0:T(8,128)(2,1)} %broadcast_select_fusion.1), channel_id=1, source_target_pairs={{0,1},{2,3},{4,5},{6,7},{9,8},{11,10},{13,12},{15,14},{16,17},{18,... | collective-permute-start | bytes 2752520 | tf_op jit(solution)/shard_map/ppermute | solution.py:32
  140.6 26.6 %collective-permute-start.42 = (bf16[448,1024]{1,0:T(8,128)(2,1)S(1)}, bf16[448,1024]{1,0:T(8,128)(2,1)S(1)}, u32[]{:S(2)}, u32[]{:S(2)}) collective-permute-start(bf16[448,1024]{1,0:T(8,128)(2,1)S(1)} %broadcast_select_fusion), channel_id=1, source_target_pairs={{0,1},{2,3},{4,5},{6,7},{9,8},{11,10},{13,12},{15,14},{16,17},{18,... | collective-permute-start | bytes 2752520 | tf_op jit(solution)/shard_map/ppermute | solution.py:32
  142.1 21.6 %collective-permute-start.32 = (bf16[224,2048]{1,0:T(8,128)(2,1)S(1)}, bf16[224,2048]{1,0:T(8,128)(2,1)S(1)}, u32[]{:S(2)}, u32[]{:S(2)}) collective-permute-start(bf16[224,2048]{1,0:T(8,128)(2,1)S(1)} %select_select_fusion.2), channel_id=1, source_target_pairs={{0,4},{1,5},{2,6},{3,7},{4,0},{5,1},{6,2},{7,3},{8,12},{9,13},{10,... | collective-permute-start | bytes 2752520 | tf_op jit(solution)/shard_map/ppermute | solution.py:32
  144.0 62.5 %collective-permute-start.10 = (bf16[4096,128]{1,0:T(8,128)(2,1)S(1)}, bf16[4096,128]{1,0:T(8,128)(2,1)S(1)}, u32[]{:S(2)}, u32[]{:S(2)}) collective-permute-start(bf16[4096,128]{1,0:T(8,128)(2,1)S(1)} %constant_dynamic-slice_fusion.3), channel_id=1, source_target_pairs={{0,1},{1,0},{2,3},{3,2},{4,5},{5,4},{6,7},{7,6},{8,9},{9,8},{10,11... | collective-permute-start | bytes 3145736 | tf_op jit(solution)/shard_map/ppermute | solution.py:32
  144.2 68.7 %collective-permute-start.15 = (bf16[112,4096]{1,0:T(8,128)(2,1)S(1)}, bf16[112,4096]{1,0:T(8,128)(2,1)S(1)}, u32[]{:S(2)}, u32[]{:S(2)}) collective-permute-start(bf16[112,4096]{1,0:T(8,128)(2,1)S(1)} %broadcast_select_fusion.9), channel_id=1, source_target_pairs={{0,2},{1,3},{2,0},{3,1},{4,6},{5,7},{6,4},{7,5},{8,10},{9,11},{10,... | collective-permute-start | bytes 2752520 | tf_op jit(solution)/shard_map/ppermute | solution.py:32
  163.7 31.5 %collective-permute-start.33 = (bf16[448,1024]{1,0:T(8,128)(2,1)S(1)}, bf16[448,1024]{1,0:T(8,128)(2,1)S(1)}, u32[]{:S(2)}, u32[]{:S(2)}) collective-permute-start(bf16[448,1024]{1,0:T(8,128)(2,1)S(1)} %fusion.36), channel_id=1, source_target_pairs={{0,2},{4,6},{9,11},{13,15},{18,16},{22,20},{27,25},{31,29}} | collective-permute-start | bytes 2752520 | tf_op jit(solution)/shard_map/ppermute | solution.py:32
  167.2 37.8 %collective-permute-start.35 = (bf16[448,1024]{1,0:T(8,128)(2,1)S(1)}, bf16[448,1024]{1,0:T(8,128)(2,1)S(1)}, u32[]{:S(2)}, u32[]{:S(2)}) collective-permute-start(bf16[448,1024]{1,0:T(8,128)(2,1)S(1)} %fusion.35), channel_id=1, source_target_pairs={{0,2},{4,6},{9,11},{13,15},{18,16},{22,20},{27,25},{31,29}} | collective-permute-start | bytes 2752520 | tf_op jit(solution)/shard_map/ppermute | solution.py:32
  195.2 24.9 %collective-permute-start.7 = (bf16[112,4096]{1,0:T(8,128)(2,1)S(1)}, bf16[112,4096]{1,0:T(8,128)(2,1)S(1)}, u32[]{:S(2)}, u32[]{:S(2)}) collective-permute-start(bf16[112,4096]{1,0:T(8,128)(2,1)S(1)} %copy-done.11), channel_id=1, source_target_pairs={{0,2},{1,3},{2,0},{3,1},{4,6},{5,7},{6,4},{7,5},{8,10},{9,11},{10,... | collective-permute-start | bytes 2752520 | tf_op jit(solution)/shard_map/ppermute | solution.py:32
  205.1 18.7 %collective-permute-start.34 = (bf16[448,1024]{1,0:T(8,128)(2,1)S(1)}, bf16[448,1024]{1,0:T(8,128)(2,1)S(1)}, u32[]{:S(2)}, u32[]{:S(2)}) collective-permute-start(bf16[448,1024]{1,0:T(8,128)(2,1)S(1)} %broadcast_select_fusion.3), channel_id=1, source_target_pairs={{0,1},{2,3},{4,5},{6,7},{9,8},{11,10},{13,12},{15,14},{16,17},{18,... | collective-permute-start | bytes 2752520 | tf_op jit(solution)/shard_map/ppermute | solution.py:32
  206.5 37.1 %collective-permute-start.36 = (bf16[448,1024]{1,0:T(8,128)(2,1)S(1)}, bf16[448,1024]{1,0:T(8,128)(2,1)S(1)}, u32[]{:S(2)}, u32[]{:S(2)}) collective-permute-start(bf16[448,1024]{1,0:T(8,128)(2,1)S(1)} %broadcast_select_fusion.2), channel_id=1, source_target_pairs={{0,1},{2,3},{4,5},{6,7},{9,8},{11,10},{13,12},{15,14},{16,17},{18,... | collective-permute-start | bytes 2752520 | tf_op jit(solution)/shard_map/ppermute | solution.py:32
  215.6 27.7 %collective-permute-start.16 = (bf16[224,640]{1,0:T(8,128)(2,1)S(1)}, bf16[224,640]{1,0:T(8,128)(2,1)S(1)}, u32[]{:S(2)}, u32[]{:S(2)}) collective-permute-start(bf16[224,640]{1,0:T(8,128)(2,1)S(1)} %get-tuple-element.21), channel_id=1, source_target_pairs={{0,16},{1,24},{2,18},{3,26},{4,20},{5,28},{6,22},{7,30},{8,17},{9,... | collective-permute-start | bytes 860168 | tf_op jit(solution)/shard_map/ppermute | solution.py:32
  222.8 20.6 %collective-permute-start.12 = (bf16[224,640]{1,0:T(8,128)(2,1)S(1)}, bf16[224,640]{1,0:T(8,128)(2,1)S(1)}, u32[]{:S(2)}, u32[]{:S(2)}) collective-permute-start(bf16[224,640]{1,0:T(8,128)(2,1)S(1)} %get-tuple-element.20), channel_id=1, source_target_pairs={{0,1},{1,9},{2,3},{3,11},{4,5},{5,13},{6,7},{7,15},{8,0},{9,8},{10... | collective-permute-start | bytes 860168 | tf_op jit(solution)/shard_map/ppermute | solution.py:32
  223.8 19.5 %collective-permute-start.11 = (bf16[224,640]{1,0:T(8,128)(2,1)S(1)}, bf16[224,640]{1,0:T(8,128)(2,1)S(1)}, u32[]{:S(2)}, u32[]{:S(2)}) collective-permute-start(bf16[224,640]{1,0:T(8,128)(2,1)S(1)} %get-tuple-element.19), channel_id=1, source_target_pairs={{1,8},{3,10},{5,12},{7,14},{8,1},{10,3},{12,5},{14,7},{17,24},{19,... | collective-permute-start | bytes 860168 | tf_op jit(solution)/shard_map/ppermute | solution.py:32
  (26 other events, 305.6 us)
